TPU v7x, 32 devices: a 4x4x1 block of a 4x4x8 slice. The times are simulated.
32 devices in a mesh: rep: 2 (over z, core), dp: 16 (over x, y).
Axes of the slice: x: 4, y: 4, z: 1, core: 2. Of those that a mesh axis runs over, the one named last changes fastest.
The devices are a block of a 4x4x8 slice.
Arguments:
- x: bfloat16 [32, 4096, 896], P(('rep', 'dp')), parts along dimension 0
- dy: bfloat16 [32, 4096, 896], P(('rep', 'dp')), parts along dimension 0
- w_gate: bfloat16 [2, 896, 2304], P(None, 'dp')
- w_up: bfloat16 [2, 896, 2304], P(None, 'dp')
- w_down: bfloat16 [2, 2304, 896], P(None, 'dp')
- m_w_gate: float32 [2, 896, 2304], P(None, 'dp')
- m_w_up: float32 [2, 896, 2304], P(None, 'dp')
- m_w_down: float32 [2, 2304, 896], P(None, 'dp')
- v_w_gate: float32 [2, 896, 2304], P(None, 'dp')
- v_w_up: float32 [2, 896, 2304], P(None, 'dp')
- v_w_down: float32 [2, 2304, 896], P(None, 'dp')
Outputs:
- output 1: bfloat16 [4, 896, 2304], P('rep', 'dp'), parts along dimension 0
- output 2: bfloat16 [4, 896, 2304], P('rep', 'dp'), parts along dimension 0
- output 3: bfloat16 [4, 2304, 896], P('rep', 'dp'), parts along dimension 0
- output 4: float32 [4, 896, 2304], P('rep', 'dp'), parts along dimension 0
- output 5: float32 [4, 896, 2304], P('rep', 'dp'), parts along dimension 0
- output 6: float32 [4, 2304, 896], P('rep', 'dp'), parts along dimension 0
- output 7: float32 [4, 896, 2304], P('rep', 'dp'), parts along dimension 0
- output 8: float32 [4, 896, 2304], P('rep', 'dp'), parts along dimension 0
- output 9: float32 [4, 2304, 896], P('rep', 'dp'), parts along dimension 0
There are 2 independent parts. A program takes and returns all parts, laid end to end along the dimension named above; an argument that names none is the same for every part.
All inputs are finite; a program needn't handle non-finite values.
Results may differ from a plain program's by a relative error of at most 0.022.
Values are sent between devices in bfloat16 or wider.
A program may use at most 768 MiB of HBM per device.

v0:
```python
import jax
import jax.numpy as jnp
from jax import lax
from jax.sharding import PartitionSpec as P

NAMES = ("w_gate", "w_up", "w_down")


def matmul(a, w):
    return jnp.dot(a, w, preferred_element_type=jnp.float32).astype(jnp.bfloat16)


def normed(h):
    wide = h.astype(jnp.float32)
    scale = lax.rsqrt(jnp.mean(wide**2, -1, keepdims=True) + 1e-6)
    return (wide * scale).astype(jnp.bfloat16)


def layer(h, w):
    a = normed(h)
    gate = jnp.dot(a, w["w_gate"], preferred_element_type=jnp.float32)
    up = jnp.dot(a, w["w_up"], preferred_element_type=jnp.float32)
    return h + matmul((jax.nn.silu(gate) * up).astype(jnp.bfloat16), w["w_down"])


def adamw(w, m, v, g):
    m = 0.9 * m + 0.1 * g
    v = 0.95 * v + 0.05 * g * g
    step = m * lax.rsqrt(v + 1e-8) + 0.1 * w
    return (w - 0.02 * step).astype(jnp.bfloat16), m, v


def clipped(gradients, sum_of_squares, count):
    factor = jnp.minimum(1.0, 0.5 * lax.rsqrt(sum_of_squares / count + 1e-30))
    return [g * factor for g in gradients]


def solution(mesh):
    def fetched(weights, number):
        return {name: lax.all_gather(w[number], "dp", axis=0, tiled=True) for name, w in zip(NAMES, weights, strict=True)}

    def step(x, dy, *arrays):
        weights, m, v = (arrays[i : i + 3] for i in (0, 3, 6))
        layers = weights[0].shape[0]
        h, kept = x[0], []
        for number in range(layers):
            kept.append(h)
            h = layer(h, fetched(weights, number))
        by_h, mine = dy[0], [None] * layers
        for number in reversed(range(layers)):
            _, back = jax.vjp(lambda w, h: layer(h, w), fetched(weights, number), kept[number])
            by_w, by_h = back(by_h)
            mine[number] = [lax.psum_scatter(by_w[name], "dp", scatter_dimension=0, tiled=True) for name in NAMES]
        gradients = [jnp.stack([mine[number][i] for number in range(layers)]).astype(jnp.float32) for i in range(3)]
        squares = lax.psum(sum(jnp.sum(g * g) for g in gradients), "dp")
        gradients = clipped(gradients, squares, lax.psum(1, "dp") * sum(g.size for g in gradients))
        new = [adamw(w.astype(jnp.float32), m, v, g) for w, m, v, g in zip(weights, m, v, gradients, strict=True)]
        return tuple(one[which] for which in range(3) for one in new)

    states, cut = P(("rep", "dp"), None, None), P(None, "dp", None)
    return jax.shard_map(
        step,
        mesh=mesh,
        in_specs=(states, states) + (cut,) * 9,
        out_specs=(P("rep", "dp", None),) * 9,
        check_vma=False,
    )
```

profile of v0, /device:TPU:96, one launch (start us, length us, event | category | flops | bytes accessed | tf_op | source)
XLA Modules:
  0.0 957.2 jit_solution(13286301072071960280)
XLA Ops:
  7.3 1.9 fusion.91
  9.2 0.1 all-gather.15.cloned.1.call-start
  9.3 1.9 fusion.90
  11.2 0.1 all-gather.17.cloned.1.call-start
  11.3 1.9 fusion.89
  13.3 0.6 all-gather.23.cloned.1.call-update
  14.0 0.6 all-gather.21.cloned.1.call-update
  14.6 0.6 all-gather.19.cloned.1.call-update
  15.3 10.8 %copy.22 = bf16[1,4096,896]{1,2,0:T(8,128)(2,1)} copy(bf16[1,4096,896]{2,1,0:T(8,128)(2,1)} %param.11) | data formatting | bytes 14680064 | tf_op args[0]
  26.0 4.6 fusion.15
  30.6 10.7 %copy.23 = bf16[1,4096,896]{1,2,0:T(8,128)(2,1)} copy(bf16[1,4096,896]{2,1,0:T(8,128)(2,1)} %param.12) | data formatting | bytes 14680064 | tf_op args[1]
  41.4 17.7 %all-gather.13.cloned.1.call-done = bf16[1,896,2304]{2,1,0:T(8,128)(2,1)} async-done(((bf16[1,56,2304]{2,1,0:T(8,128)(2,1)}), bf16[1,896,2304]{2,1,0:T(8,128)(2,1)}) %all-gather.13.cloned.1.call-update) | async-done | bytes 4128784 | tf_op jit(solution)/shard_map/all_gather | solution.py:40
  59.0 26.9 %fusion.44 = f32[4096,2304]{1,0:T(8,128)} fusion(bf16[1,4096,896]{1,2,0:T(8,128)(2,1)} %copy.22, f32[4096]{0:T(1024)S(1)} %add_rsqrt_fusion, bf16[1,896,2304]{2,1,0:T(8,128)(2,1)} %all-gather.13.cloned.1.call-done), kind=kOutput, calls=%fused_computation.54 | convolution fusion | flops 16922443776 | bytes 49233920 | tf_op jit(solution)/shard_map/dot_general | solution.py:21
  86.0 21.0 %all-gather.15.cloned.1.call-done = bf16[1,896,2304]{2,1,0:T(8,128)(2,1)} async-done(((bf16[1,56,2304]{2,1,0:T(8,128)(2,1)}), bf16[1,896,2304]{2,1,0:T(8,128)(2,1)}) %all-gather.15.cloned.1.call-update) | async-done | bytes 4128784 | tf_op jit(solution)/shard_map/all_gather | solution.py:40
  106.9 41.9 %multiply_convert_fusion.1 = (bf16[4096,2304]{1,0:T(8,128)(2,1)}, f32[4096,2304]{1,0:T(8,128)}) fusion(f32[4096,2304]{1,0:T(8,128)} %fusion.44, bf16[1,896,2304]{2,1,0:T(8,128)(2,1)} %all-gather.15.cloned.1.call-done, bf16[1,4096,896]{1,2,0:T(8,128)(2,1)} %copy.22, f32[4096]{0:T(1024)S(1)} %add_rsqrt_fusion), kind=kOutput, calls=%fused_computation.17 | convolution fusion | flops 16979066880 | bytes 105857024 | tf_op jit(solution)/shard_map/dot_general | solution.py:22
  148.9 6.0 all-gather.17.cloned.1.call-done
  154.8 24.4 %fusion.19 = (f32[4096]{0:T(1024)S(1)}, bf16[4096,896]{0,1:T(8,128)(2,1)}) fusion(bf16[4096,2304]{1,0:T(8,128)(2,1)} %get-tuple-element.24, bf16[1,2304,896]{2,1,0:T(8,128)(2,1)} %all-gather.17.cloned.1.call-done, bf16[1,4096,896]{1,2,0:T(8,128)(2,1)} %copy.22), kind=kOutput, calls=%fused_computation.37 | convolution fusion | flops 16929779712 | bytes 37699584 | tf_op jit(solution)/shard_map/dot_general | solution.py:10
  179.3 0.6 copy-done.7
  179.9 22.7 %all-gather.23.cloned.1.call-done = bf16[1,896,2304]{2,1,0:T(8,128)(2,1)} async-done(((bf16[1,56,2304]{2,1,0:T(8,128)(2,1)}), bf16[1,896,2304]{2,1,0:T(8,128)(2,1)}) %all-gather.23.cloned.1.call-update) | async-done | bytes 4128784 | tf_op jit(solution)/shard_map/all_gather | solution.py:40
  202.6 27.1 %fusion.36 = f32[4096,2304]{1,0:T(8,128)} fusion(bf16[4096,896]{0,1:T(8,128)(2,1)} %get-tuple-element.27, f32[4096]{0:T(1024)S(1)} %fusion.77, bf16[1,896,2304]{2,1,0:T(8,128)(2,1)} %all-gather.23.cloned.1.call-done), kind=kOutput, calls=%fused_computation.51 | convolution fusion | flops 16922443776 | bytes 49233920 | tf_op jit(solution)/shard_map/jvp()/dot_general | solution.py:22
  229.6 20.7 %all-gather.21.cloned.1.call-done = bf16[1,2304,896]{2,1,0:T(8,128)(2,1)} async-done(((bf16[1,144,896]{2,1,0:T(8,128)(2,1)}), bf16[1,2304,896]{2,1,0:T(8,128)(2,1)}) %all-gather.21.cloned.1.call-update) | async-done | bytes 4128784 | tf_op jit(solution)/shard_map/all_gather | solution.py:40
  250.3 26.6 %convolution_convert_fusion.1 = bf16[4096,2304]{1,0:T(8,128)(2,1)} fusion(bf16[1,4096,896]{2,1,0:T(8,128)(2,1)} %param.12, bf16[1,2304,896]{2,1,0:T(8,128)(2,1)} %all-gather.21.cloned.1.call-done), kind=kOutput, calls=%fused_computation.27 | convolution fusion | flops 16920870912 | bytes 30343168 | tf_op jit(solution)/shard_map/transpose(jvp())/dot_general | solution.py:10
  276.9 21.2 %all-gather.19.cloned.1.call-done = bf16[1,896,2304]{2,1,0:T(8,128)(2,1)} async-done(((bf16[1,56,2304]{2,1,0:T(8,128)(2,1)}), bf16[1,896,2304]{2,1,0:T(8,128)(2,1)}) %all-gather.19.cloned.1.call-update) | async-done | bytes 4128784 | tf_op jit(solution)/shard_map/all_gather | solution.py:40
  298.1 52.0 %fusion.2 = (bf16[4096,2304]{1,0:T(8,128)(2,1)}, f32[4096,2304]{1,0:T(8,128)}) fusion(f32[4096,2304]{1,0:T(8,128)} %fusion.36, bf16[4096,2304]{1,0:T(8,128)(2,1)} %convolution_convert_fusion.1, bf16[1,896,2304]{2,1,0:T(8,128)(2,1)} %all-gather.19.cloned.1.call-done, bf16[4096,896]{0,1:T(8,128)(2,1)} %get-tuple-element.27, f32[4096]{0:T(1024)S(1)} %fusion.77), kind=kOutput, calls=%fused_computation.8 | convolution fusion | flops 17035689984 | bytes 124731392 | tf_op jit(solution)/shard_map/jvp()/dot_general | solution.py:21
  350.1 22.8 %fusion.49 = bf16[4096,896]{0,1:T(8,128)(2,1)} fusion(bf16[4096,2304]{1,0:T(8,128)(2,1)} %get-tuple-element.28, bf16[1,896,2304]{2,1,0:T(8,128)(2,1)} %all-gather.19.cloned.1.call-done), kind=kOutput, calls=%fused_computation.58 | convolution fusion | flops 16911433728 | bytes 30343168 | tf_op jit(solution)/shard_map/transpose(jvp())/dot_general | solution.py:21
  372.9 35.2 %fusion.21 = (f32[4096]{0:T(1024)S(1)}, bf16[4096,896]{0,1:T(8,128)(2,1)}) fusion(bf16[4096,896]{0,1:T(8,128)(2,1)} %get-tuple-element.27, bf16[4096,896]{0,1:T(8,128)(2,1)} %fusion.49, bf16[1,896,2304]{2,1,0:T(8,128)(2,1)} %all-gather.23.cloned.1.call-done, bf16[4096,2304]{1,0:T(8,128)(2,1)} %convolution_convert_fusion.1, f32[4096,2304]{1,0:T(8,128)} %get-tuple-element.29), kind=kOutput, calls=%fused_computation.39 | convolution fusion | flops 16990072832 | bytes 82788352 | tf_op jit(solution)/shard_map/transpose(jvp())/dot_general | solution.py:22
  408.2 9.8 %fusion.22 = bf16[4096,896]{0,1:T(8,128)(2,1)S(1)} fusion(bf16[4096,896]{0,1:T(8,128)(2,1)} %get-tuple-element.27, bf16[4096,896]{0,1:T(8,128)(2,1)} %get-tuple-element.31, bf16[1,4096,896]{1,2,0:T(8,128)(2,1)} %copy.23, f32[4096]{0:T(1024)S(1)} %multiply_multiply_fusion.3, f32[4096]{0:T(1024)S(1)} %fusion.77), kind=kLoop, calls=%fused_computation.40 | loop fusion | flops 25690112 | bytes 29392896 | tf_op jit(solution)/shard_map/transpose(jvp())/add_any | solution.py:14
  418.0 2.9 copy-done
  420.9 24.1 %convolution_convert_fusion.2 = bf16[2304,896]{1,0:T(8,128)(2,1)} fusion(bf16[4096,2304]{1,0:T(8,128)(2,1)} %get-tuple-element.24, bf16[4096,896]{0,1:T(8,128)(2,1)S(1)} %fusion.22), kind=kOutput, calls=%fused_computation.49 | convolution fusion | flops 16913498112 | bytes 30343168 | tf_op jit(solution)/shard_map/transpose(jvp())/dot_general | solution.py:10
  445.1 0.1 reduce-scatter.29.cloned.1.call-start
  445.2 34.0 %fusion.26 = bf16[2304,896]{1,0:T(8,128)(2,1)} fusion(bf16[1,4096,896]{2,1,0:T(8,128)(2,1)} %param.12, f32[4096,2304]{1,0:T(8,128)} %fusion.36, f32[4096,2304]{1,0:T(8,128)} %get-tuple-element.29), kind=kOutput, calls=%fused_computation.45 | convolution fusion | flops 16970121216 | bytes 86966272 | tf_op jit(solution)/shard_map/transpose(jvp())/dot_general | solution.py:10
  479.3 0.1 reduce-scatter.23.cloned.1.call-start
  479.4 27.3 %convolution_convert_fusion = bf16[4096,2304]{1,0:T(8,128)(2,1)} fusion(bf16[4096,896]{0,1:T(8,128)(2,1)} %copy-done, bf16[1,2304,896]{2,1,0:T(8,128)(2,1)} %all-gather.17.cloned.1.call-done), kind=kOutput, calls=%fused_computation.26 | convolution fusion | flops 16920870912 | bytes 30343168 | tf_op jit(solution)/shard_map/transpose(jvp())/dot_general | solution.py:10
  506.7 34.3 %fusion.33 = bf16[896,2304]{1,0:T(8,128)(2,1)} fusion(bf16[4096,2304]{1,0:T(8,128)(2,1)} %convolution_convert_fusion, f32[4096,2304]{1,0:T(8,128)} %fusion.44, bf16[1,4096,896]{1,2,0:T(8,128)(2,1)} %copy.22, f32[4096]{0:T(1024)S(1)} %copy-done.10), kind=kOutput, calls=%fused_computation.48 | convolution fusion | flops 16981131264 | bytes 68108288 | tf_op jit(solution)/shard_map/transpose(jvp())/dot_general | solution.py:22
  541.1 0.1 reduce-scatter.25.cloned.1.call-start
  541.1 34.1 %fusion.29 = bf16[896,2304]{1,0:T(8,128)(2,1)} fusion(bf16[4096,2304]{1,0:T(8,128)(2,1)} %convolution_convert_fusion.1, bf16[4096,896]{0,1:T(8,128)(2,1)} %get-tuple-element.27, f32[4096]{0:T(1024)S(1)} %copy-done.6, f32[4096,2304]{1,0:T(8,128)} %get-tuple-element.29), kind=kOutput, calls=%fused_computation.46 | convolution fusion | flops 16981131264 | bytes 68108288 | tf_op jit(solution)/shard_map/transpose(jvp())/dot_general | solution.py:22
  575.3 39.4 %fusion.30 = bf16[896,2304]{1,0:T(8,128)(2,1)} fusion(f32[4096,2304]{1,0:T(8,128)} %fusion.44, f32[4096,2304]{1,0:T(8,128)} %get-tuple-element.25, bf16[4096,2304]{1,0:T(8,128)(2,1)} %convolution_convert_fusion, bf16[1,4096,896]{1,2,0:T(8,128)(2,1)} %copy.22, f32[4096]{0:T(1024)S(1)} %copy-done.10), kind=kOutput, calls=%fused_computation.47 | convolution fusion | flops 17028317184 | bytes 105857024 | tf_op jit(solution)/shard_map/transpose(jvp())/dot_general | solution.py:21
  614.9 24.1 %convolution_convert_fusion.3 = bf16[896,2304]{1,0:T(8,128)(2,1)} fusion(bf16[4096,2304]{1,0:T(8,128)(2,1)} %get-tuple-element.28, bf16[4096,896]{0,1:T(8,128)(2,1)} %get-tuple-element.27, f32[4096]{0:T(1024)S(1)} %copy-done.6), kind=kOutput, calls=%fused_computation.50 | convolution fusion | flops 16922443776 | bytes 30359552 | tf_op jit(solution)/shard_map/transpose(jvp())/dot_general | solution.py:21
  639.1 1.9 fusion.67
  641.0 29.3 %reduce-scatter.23.cloned.1.call-done = bf16[56,2304]{1,0:T(8,128)(2,1)} async-done(((bf16[896,2304]{1,0:T(8,128)(2,1)}), bf16[56,2304]{1,0:T(8,128)(2,1)}) %reduce-scatter.23.cloned.1.call-update) | async-done | bytes 258064
  670.4 75.9 %reduce-scatter.25.cloned.1.call-done = bf16[56,2304]{1,0:T(8,128)(2,1)} async-done(((bf16[896,2304]{1,0:T(8,128)(2,1)}), bf16[56,2304]{1,0:T(8,128)(2,1)}) %reduce-scatter.25.cloned.1.call-update) | async-done | bytes 258064
  746.2 1.9 fusion.66
  748.2 74.1 %reduce-scatter.19.cloned.1.call-done = bf16[56,2304]{1,0:T(8,128)(2,1)} async-done(((bf16[896,2304]{1,0:T(8,128)(2,1)}), bf16[56,2304]{1,0:T(8,128)(2,1)}) %reduce-scatter.19.cloned.1.call-update) | async-done | bytes 258064
  822.3 75.9 %reduce-scatter.21.cloned.1.call-done = bf16[56,2304]{1,0:T(8,128)(2,1)} async-done(((bf16[896,2304]{1,0:T(8,128)(2,1)}), bf16[56,2304]{1,0:T(8,128)(2,1)}) %reduce-scatter.21.cloned.1.call-update) | async-done | bytes 258064
  898.2 1.9 fusion.65
  902.1 38.7 %psum.7 = f32[]{:T(128)} all-reduce(f32[]{:T(128)S(6)} %add.99), channel_id=1, replica_groups=mesh['rep'=2,'dp'=16] {'dp'}, use_global_device_ids=true, to_apply=%region_12.13 | all-reduce | flops 1 | bytes 8 | tf_op jit(solution)/shard_map/psum | solution.py:55
  941.4 3.5 fusion.73
  945.0 5.1 fusion.64
  (41 shorter events, 1.1 us)
Async XLA Ops:
  7.2 51.8 %all-gather.13.cloned.1.call-start = ((), (), s32[]{:S(2)}) async-start(), calls=%async_computation.6 | async-start | bytes 4386816 | tf_op jit(solution)/shard_map/all_gather | solution.py:40
  9.2 97.7 %all-gather.15.cloned.1.call-start = ((), (), s32[]{:S(2)}) async-start(), calls=%async_computation.7 | async-start | bytes 4386816 | tf_op jit(solution)/shard_map/all_gather | solution.py:40
  11.2 143.6 %all-gather.17.cloned.1.call-start = ((), (), s32[]{:S(2)}) async-start(), calls=%async_computation.8 | async-start | bytes 4386816 | tf_op jit(solution)/shard_map/all_gather | solution.py:40
  13.3 189.3 %all-gather.23.cloned.1.call-start = ((), (), s32[]{:S(2)}) async-start(), calls=%async_computation.11 | async-start | bytes 4386816 | tf_op jit(solution)/shard_map/all_gather | solution.py:40
  13.9 236.4 %all-gather.21.cloned.1.call-start = ((), (), s32[]{:S(2)}) async-start(), calls=%async_computation.10 | async-start | bytes 4386816 | tf_op jit(solution)/shard_map/all_gather | solution.py:40
  14.6 283.5 %all-gather.19.cloned.1.call-start = ((), (), s32[]{:S(2)}) async-start(), calls=%async_computation.9 | async-start | bytes 4386816 | tf_op jit(solution)/shard_map/all_gather | solution.py:40
  15.2 623.9 %reduce-scatter.27.cloned.1.call-start = ((), (), s32[]{:S(2)}) async-start(), calls=%async_computation.16 | async-start | bytes 4386816
  30.6 76.3 %copy-start.9 = (f32[4096]{0:T(1024)}, f32[4096]{0:T(1024)S(1)}, u32[]{:S(2)}) copy-start(f32[4096]{0:T(1024)S(1)} %add_rsqrt_fusion) | copy-start | bytes 49156
  179.3 0.6 copy-start.7
  179.9 228.3 %copy-start.5 = (f32[4096]{0:T(1024)}, f32[4096]{0:T(1024)S(1)}, u32[]{:S(2)}) copy-start(f32[4096]{0:T(1024)S(1)} %fusion.77) | copy-start | bytes 49156
  372.9 35.2 %copy-start.8 = (f32[4096]{0:T(1024)S(1)}, f32[4096]{0:T(1024)}, u32[]{:S(2)}) copy-start(f32[4096]{0:T(1024)} %copy-done.7) | copy-start | bytes 49156
  418.0 2.9 copy-start
  445.1 194.0 %reduce-scatter.29.cloned.1.call-start = ((), (), s32[]{:S(2)}) async-start(), calls=%async_computation.17 | async-start | bytes 4386816
  479.3 27.4 %copy-start.10 = (f32[4096]{0:T(1024)S(1)}, f32[4096]{0:T(1024)}, u32[]{:S(2)}) copy-start(f32[4096]{0:T(1024)} %copy-done.9) | copy-start | bytes 49156
  479.3 191.1 %reduce-scatter.23.cloned.1.call-start = ((), (), s32[]{:S(2)}) async-start(), calls=%async_computation.14 | async-start | bytes 4386816
  506.7 34.5 %copy-start.6 = (f32[4096]{0:T(1024)S(1)}, f32[4096]{0:T(1024)}, u32[]{:S(2)}) copy-start(f32[4096]{0:T(1024)} %copy-done.5) | copy-start | bytes 49156
  541.1 205.2 %reduce-scatter.25.cloned.1.call-start = ((), (), s32[]{:S(2)}) async-start(), calls=%async_computation.15 | async-start | bytes 4386816
  575.3 247.0 %reduce-scatter.19.cloned.1.call-start = ((), (), s32[]{:S(2)}) async-start(), calls=%async_computation.12 | async-start | bytes 4386816
  614.8 326.6 %copy-start.1 = (bf16[2,144,896]{2,1,0:T(8,128)(2,1)S(1)}, bf16[2,144,896]{2,1,0:T(8,128)(2,1)}, u32[]{:S(2)}) copy-start(bf16[2,144,896]{2,1,0:T(8,128)(2,1)} %param.15) | copy-start | bytes 1548292
  614.8 330.2 %copy-start.2 = (bf16[2,56,2304]{2,1,0:T(8,128)(2,1)S(1)}, bf16[2,56,2304]{2,1,0:T(8,128)(2,1)}, u32[]{:S(2)}) copy-start(bf16[2,56,2304]{2,1,0:T(8,128)(2,1)} %param.13) | copy-start | bytes 1548292
  614.8 330.2 %copy-start.3 = (bf16[2,56,2304]{2,1,0:T(8,128)(2,1)S(1)}, bf16[2,56,2304]{2,1,0:T(8,128)(2,1)}, u32[]{:S(2)}) copy-start(bf16[2,56,2304]{2,1,0:T(8,128)(2,1)} %param.14) | copy-start | bytes 1548292
  614.8 330.1 %copy-start.4 = (f32[2,56,2304]{2,1,0:T(8,128)S(1)}, f32[2,56,2304]{2,1,0:T(8,128)}, u32[]{:S(2)}) copy-start(f32[2,56,2304]{2,1,0:T(8,128)} %param.19) | copy-start | bytes 3096580
  614.8 283.3 %reduce-scatter.21.cloned.1.call-start = ((), (), s32[]{:S(2)}) async-start(), calls=%async_computation.13 | async-start | bytes 4386816
Sparse Core Ops, SparseCore 0:
  10.6 48.3 all-gather.12
  61.6 45.2 all-gather.14
  109.5 45.2 all-gather.16
  157.3 45.2 all-gather.22
  205.0 45.2 all-gather.20
  252.8 45.2 all-gather.18
  445.2 72.8 reduce-scatter.26
  521.4 72.8 reduce-scatter.28
  597.5 72.8 reduce-scatter.22
  673.4 72.7 reduce-scatter.24
  749.4 72.8 reduce-scatter.18
  825.4 72.7 reduce-scatter.20
where the time goes:
time: 964 us; the launch traced here: 957 us
  matrix products  474 us (49%)
  waiting for transfers between devices  367 us (38%)
  blocking collectives  38.7 us (4%)
  local copies, waits for them, and re-layouts  30.8 us (3%)
  other arithmetic  28.9 us (3%)
  between operations  17.2 us (2%)
    unnamed x18, waiting for transfers between devices  257 us
    dot_general x5, matrix products, layer(): up = jnp.dot(a, w['w_up'], preferred_element_type=jnp.float32)  173 us
    dot_general x5, matrix products, layer(): gate = jnp.dot(a, w['w_gate'], preferred_element_type=jnp.float32)  165 us
    dot_general x5, matrix products, matmul(): jnp.dot(a, w, preferred_element_type=jnp.float32).astype(jnp.bfloat16)  136 us
    all_gather x6, waiting for transfers between devices, fetched(): lax.all_gather(w[number], 'dp', axis=0, tiled=True)  109 us
    psum x1, blocking collectives, step(): squares = lax.psum(sum((jnp.sum(g * g) for g in gradients)), 'dp')  38.7 us
    unnamed x24, local copies, waits for them, and re-layouts  25.1 us
  transfers between devices with their start and end apart: 12, of which 10 were waited for; matrix products, arithmetic and copies ran while one was open for 39% of the time, Pallas kernels for 0%

commit v1 on v0

v1 whole, which is shorter than its diff:
```python
import math

import jax
import jax.numpy as jnp
from jax import lax
from jax.experimental import pallas as pl
from jax.experimental.pallas import tpu as pltpu
from jax.sharding import PartitionSpec as P

bf16, f32 = jnp.bfloat16, jnp.float32
MESH = pl.DeviceIdType.MESH
CH = 256
TB = 2048
TD = 2 * CH
TILE = SUB, LANES = 8, 128
PACK = 2 * SUB
WIDE = 2 * CH
VMEM_BYTES = 67043328
AHEAD = 4
SLOTS = HALVES = KINDS = PAIR = 2
NN = (((1,), (0,)), ((), ()))
NT = (((1,), (1,)), ((), ()))
TN = (((0,), (0,)), ((), ()))


def dot(a, b, dims=NN):
    return lax.dot_general(a, b, dims, preferred_element_type=f32)


def adamw_kernel(count, squares, *refs):
    groups = len(refs) // 11
    arrays, out, held, sems = refs[: groups * 4], refs[groups * 4 : groups * 7], refs[groups * 7 : -1], refs[-1]
    for i, (array, here) in enumerate(zip(arrays, held, strict=True)):
        pltpu.make_async_copy(array, here, sems.at[i]).start()
    total = jnp.sum(squares[...], keepdims=True)
    factor = jnp.minimum(1.0, 0.5 * lax.rsqrt(total / count + 1e-30))
    stores = []
    for group in range(groups):
        g_ref, w_ref, m_ref, v_ref = held[group * 4 : group * 4 + 4]
        for i in range(group * 4, group * 4 + 4):
            pltpu.make_async_copy(arrays[i], held[i], sems.at[i]).wait()
        def one_layer(at, _):
            g = g_ref[at].astype(f32) * factor
            w = w_ref[at].astype(f32)
            m = 0.9 * m_ref[at] + 0.1 * g
            v = 0.95 * v_ref[at] + 0.05 * g * g
            step = m * lax.rsqrt(v + 1e-8) + 0.1 * w
            w_ref[at] = (w - 0.02 * step).astype(bf16)
            m_ref[at] = m
            v_ref[at] = v
            return 0

        lax.fori_loop(0, g_ref.shape[0], one_layer, 0)
        for i, here in enumerate((w_ref, m_ref, v_ref)):
            stores.append(pltpu.make_async_copy(here, out[group * 3 + i], sems.at[group * 4 + i]))
            stores[-1].start()
    for copy in stores:
        copy.wait()


def step_kernel(n, x, dy, wg, wu, wd, *refs):
    (gg_h, gu_h, gd_h, ss, wgu_h, wd_h, st_h, hid_h, a0_h, h1_h, rA) = refs[:11]
    (gg, gu, gd, act, stage, wcomb, wdc, scl, acc, sst, ssr, lb, l2) = refs[11:24]
    (sx, sw, swd, s_stage, shid, sm, ag_loc, ag_s, ag_r, rs_s, rs_r, rs_l, ss_s, ss_r) = refs[24:]
    L, R, FF = wg.shape
    RF, D = wd.shape[1:]
    T = x.shape[0]
    S = math.isqrt(n)
    NC = FF // CH
    NI = L * NC
    NJ = T // TB
    NB = T // TD
    NW = 3
    HW = RF // 2 // NW
    RC = RF // NC
    RB = R + SUB * pl.cdiv(D, CH)
    me, rep = lax.axis_index("dp"), lax.axis_index("rep")
    px, py = me // S, me % S
    par = rep % SLOTS
    one_chunk = wgu_h.at[0, 0, 0]
    partner = {"rep": rep + 1 - 2 * par, "dp": me}
    aT, dyT = act.at[0], act.at[1]
    vmem = pltpu.VMEM

    def at(ix, iy):
        return {"dp": (ix % S) * S + iy % S}

    def send(src, dst, s, r, to):
        pltpu.make_async_remote_copy(src_ref=src, dst_ref=dst, send_sem=s, recv_sem=r, device_id=to, device_id_type=MESH).start()

    def wait(ref, sem):
        pltpu.make_async_copy(ref, ref, sem).wait()

    def cols(c):
        return pl.ds(pl.multiple_of(c * CH, CH), CH)

    def blocks(b, size):
        return pl.ds(pl.multiple_of(b * size, size), size)

    def load_w(i, slot):
        for h in range(HALVES):
            pltpu.make_async_copy(wgu_h.at[h, i // NC, i % NC], wcomb.at[slot, :, :, :, pl.ds(h * CH, CH)], sw.at[slot, h]).start()

    def wait_w(slot):
        for h in range(HALVES):
            wait(one_chunk, sw.at[slot, h])

    def load_wd(l, c, slot):
        return pltpu.make_async_copy(wd_h.at[l, cols(c)], wdc.at[slot], swd.at[slot])

    def item(k):
        return L - 1 - k // NC, k % NC

    def load_stage(k, j):
        l, c = item(k)
        return pltpu.make_async_copy(st_h.at[l, c, :, blocks(j, TB)], stage.at[j], s_stage.at[j])

    def norm(src, dst):
        def rows(g):
            return pl.ds(g * PACK, PACK)

        total = jnp.zeros((SUB, src.shape[1]), f32)
        for g in range(D // (PACK)):
            wide = src[rows(g), :].astype(f32)
            wide = wide * wide
            total += wide[:SUB] + wide[SUB:]
        scale = lax.rsqrt(jnp.sum(total, axis=0, keepdims=True) / D + 1e-6)
        for g in range(D // (PACK)):
            dst[rows(g), :] = (src[rows(g), :].astype(f32) * scale).astype(bf16)
        return scale

    def forward(hiddenT, w_down, xs, dys, h1s, wl, wdl, sh, sdy):
        def with_down(i):
            return pl.when((i % NC >= NW) & (i % NC % PAIR == 1))

        def rows(d, c):
            return pl.ds(pl.multiple_of(d * RF + par * (RF // 2) + (c - NW) // PAIR * HW, 8), HW)

        def ag1(i):
            l, c = i // NC, i % NC
            p = i % AHEAD
            src, own = wl.at[par, l, :, cols(c)], wgu_h.at[par, l, c, px, py]
            for r in range(1, S):
                send(src, own, ag_s.at[0, p, 0], ag_r.at[0, i, 0], at(px + r * (1 - par), py + r * par))
            pltpu.make_async_copy(src, own, ag_loc.at[p, 0]).start()

            @with_down(i)
            def _():
                src, own = wdl.at[l, par * NW + (c - NW) // PAIR], wd_h.at[l, rows(me, c)]
                for r in range(1, S):
                    send(src, own, ag_s.at[0, p, 1], ag_r.at[0, i, 1], at(px + r * (1 - par), py + r * par))
                pltpu.make_async_copy(src, own, ag_loc.at[p, 1]).start()

        def ag2(i):
            l, c = i // NC, i % NC
            p = i % AHEAD
            for sem in (ag_r.at[0, i, 0], ag_s.at[0, p, 0]):
                wait(wgu_h.at[0, 0, 0, 0, pl.ds(0, S - 1)], sem)
            wait(wgu_h.at[0, 0, 0, 0, 0], ag_loc.at[p, 0])

            @pl.when(par == 0)
            def _():
                w = wgu_h.at[0, l, c, :, py]
                for r in range(1, S):
                    send(w, w, ag_s.at[1, p, 0], ag_r.at[1, i, 0], at(px, py + r))

            @pl.when(par == 1)
            def _():
                w = wgu_h.at[1, l, c, px]
                for r in range(1, S):
                    send(w, w, ag_s.at[1, p, 0], ag_r.at[1, i, 0], at(px + r, py))

            @with_down(i)
            def _():
                for sem in (ag_r.at[0, i, 1], ag_s.at[0, p, 1]):
                    wait(wd_h.at[0, pl.ds(0, (S - 1) * HW)], sem)
                wait(wd_h.at[0, pl.ds(0, HW)], ag_loc.at[p, 1])
                for k in range(S):
                    v = wd_h.at[l, rows((1 - par) * (S * k + py) + par * (S * px + k), c)]
                    for r in range(1, S):
                        send(v, v, ag_s.at[1, p, 1], ag_r.at[1, i, 1], at(px + r * par, py + r * (1 - par)))

        def ag3(i):
            l, c = i // NC, i % NC
            p = i % AHEAD
            for sem in (ag_r.at[1, i, 0], ag_s.at[1, p, 0]):
                wait(wgu_h.at[0, 0, 0, pl.ds(0, S - 1)], sem)
            w = wgu_h.at[par, l, c]
            send(w, w, ag_s.at[2, p, 0], ag_r.at[2, i, 0], partner)

            @with_down(i - 1)
            def _():
                for sem in (ag_r.at[1, i - 1, 1], ag_s.at[1, (i - 1) % AHEAD, 1]):
                    wait(wd_h.at[0, pl.ds(0, S * (S - 1) * HW)], sem)
                for d in range(n):
                    v = wd_h.at[l, rows(d, (i - 1) % NC)]
                    send(v, v, ag_s.at[2, (i - 1) % AHEAD, 1], ag_r.at[2, i - 1, 1], partner)

        def ag4(i):
            for sem in (ag_r.at[2, i, 0], ag_s.at[2, i % AHEAD, 0]):
                wait(one_chunk, sem)

            @with_down(i - 1)
            def _():
                for sem in (ag_r.at[2, i - 1, 1], ag_s.at[2, (i - 1) % AHEAD, 1]):
                    wait(wd_h.at[0, pl.ds(0, n * HW)], sem)

        pltpu.make_async_copy(wg, wl.at[0], sm.at[0]).start()
        pltpu.make_async_copy(wu, wl.at[1], sm.at[1]).start()
        for l in range(L):
            for q in range(RF // HW):
                pltpu.make_async_copy(wd.at[l, pl.ds(q * HW, HW)], wdl.at[l, q], sm.at[2]).start()
        barrier = pltpu.get_barrier_semaphore()
        for r in range(1, n):
            pl.semaphore_signal(barrier, inc=1, device_id={"dp": (me + r) % n}, device_id_type=MESH)
        pl.semaphore_signal(barrier, inc=1, device_id=partner, device_id_type=MESH)

        def fetch(b):
            return pltpu.make_async_copy(x.at[blocks(b, TD)], xs.at[b % SLOTS], sx.at[b % SLOTS])

        def turn(b, _):
            pl.when(b + 1 < NB)(lambda: fetch(b + 1).start())
            fetch(b).wait()
            aT[:, blocks(b, TD)] = xs[b % SLOTS].T
            before = blocks((b + NB - 1) % NB, TD)
            norm(aT.at[:, before], aT.at[:, before])
            return 0

        fetch(0).start()
        wait(wl.at[0], sm.at[0])
        wait(wl.at[1], sm.at[1])
        wait(wdl, sm.at[2])
        pl.semaphore_wait(barrier, n)
        for i in range(3):
            ag1(i)
        lax.fori_loop(0, 3, turn, 0)
        ag2(0)
        lax.fori_loop(3, 4, turn, 0)
        ag2(1)
        ag2(2)
        ag1(3)
        lax.fori_loop(4, NB, turn, 0)
        norm(aT.at[:, blocks(NB - 1, TD)], aT.at[:, blocks(NB - 1, TD)])
        acc[...] = jnp.zeros_like(acc)
        ag3(0)
        ag4(0)
        load_w(0, 0)
        pltpu.make_async_copy(aT, a0_h, sm.at[0]).start()
        ag3(1)

        def load_down(third):
            some = blocks(third, FF // NW)
            return pltpu.make_async_copy(wd_h.at[0, some], w_down.at[some], swd.at[0])

        def down():
            fetch(0).start()
            for third in range(NW):
                load_down(third).wait()
            wait(aT, sm.at[0])

            def save(b):
                return pltpu.make_async_copy(h1s.at[b % SLOTS], h1_h.at[:, blocks(b, TD)], sh.at[b % SLOTS])

            def normed(b):
                scl[:, blocks(b, TD)] = norm(h1s.at[b % SLOTS], aT.at[:, blocks(b, TD)])

            def block(b, _):
                @pl.when(b + 1 < NB)
                def _():
                    fetch(b + 1).start()

                fetch(b).wait()
                pl.when(b >= 2)(lambda: save(b - 2).wait())
                out = dot(w_down[...], hiddenT[:, blocks(b, TD)], TN).astype(bf16)
                normed((b + NB - 1) % NB)
                h1s[b % SLOTS] = xs[b % SLOTS].T + out
                save(b).start()
                return 0

            lax.fori_loop(0, NB, block, 0)
            normed(NB - 1)
            for b in range(NB - 2, NB):
                save(b).wait()

        def save_hidden(i):
            return pltpu.make_async_copy(hiddenT.at[cols(i % NC)], hid_h.at[i // NC, cols(i % NC)], shid.at[i % SLOTS])

        def part_of_dy(q):
            return q % (T // LANES)

        def fetch_dy(q):
            return pltpu.make_async_copy(dy.at[pl.ds(pl.multiple_of(part_of_dy(q) * LANES, LANES), LANES)], dys.at[q % SLOTS], sdy.at[q % SLOTS])

        fetch_dy(0).start()

        def chunk(i, _):
            l, c = i // NC, i % NC
            pl.when((c == 0) & (l > 0))(down)
            slot = i % SLOTS
            wait_w(slot)
            pl.when(i + 3 < NI)(lambda: ag2(i + 3))
            pl.when(i + 4 < NI)(lambda: ag1(i + 4))

            @pl.when(i == NC - 1)
            def _():
                for third in range(NW):
                    load_down(third).start()

            def block(j, _):
                @pl.when((j == NJ - 1) & (i + 1 < NI))
                def _():
                    ag4(i + 1)
                    load_w(i + 1, 1 - slot)

                pl.when((j == NJ - 1) & (i + 2 < NI))(lambda: ag3(i + 2))
                q = i * NJ + j
                pl.when(q + 1 < NI * NJ)(lambda: fetch_dy(q + 1).start())
                fetch_dy(q).wait()

                @pl.when(i > 0)
                def _():
                    wait(stage.at[j], s_stage.at[j])

                t = blocks(j, TB)
                r = dot(wcomb[slot].reshape(D, WIDE), aT[:, t], TN)
                gate, up = r[:CH], r[CH:]
                sig = 0.5 * jnp.tanh(0.5 * gate) + 0.5
                silu = gate * sig
                stage[j, :CH, :] = silu
                stage[j, CH:, :] = up * (sig + silu * (1.0 - sig))
                hiddenT[cols(c), t] = (silu * up).astype(bf16)
                dyT[:, pl.ds(pl.multiple_of(part_of_dy(q) * LANES, LANES), LANES)] = dys[q % SLOTS].T
                pltpu.make_async_copy(stage.at[j], st_h.at[l, c, :, t], s_stage.at[j]).start()
                return 0

            lax.fori_loop(0, NJ, block, 0)
            pl.when(i >= 2)(lambda: save_hidden(i - 2).wait())
            save_hidden(i).start()
            return 0

        lax.fori_loop(0, NI, chunk, 0)
        load_wd(*item(0), 0).start()
        for j in range(NJ):
            wait(stage.at[j], s_stage.at[j])
            load_stage(0, j).start()
        load_w(item(0)[0] * NC + item(0)[1], 0)
        for i in range(NI - SLOTS, NI):
            save_hidden(i).wait()

    dma = pltpu.SemaphoreType.DMA
    pl.run_scoped(
        forward,
        vmem((FF, T), bf16),
        vmem((FF, D), bf16),
        vmem((SLOTS, TD, D), bf16),
        vmem((SLOTS, LANES, D), bf16),
        vmem((SLOTS, D, TD), bf16),
        vmem((SLOTS, L, R, FF), bf16),
        vmem((L, RF // HW, HW, D), bf16),
        dma((SLOTS,)),
        dma((SLOTS,)),
    )

    def backward(daT, big, hid, Fg, Fd, s1, sb, s2, o1, o2, la, sh):
        pieces = [(pl.ds(0, R), pl.ds(0, CH))] + [(pl.ds(R + i * SUB, SUB), pl.ds(0, min(CH, D - i * CH))) for i in range(pl.cdiv(D, CH))]

        def down_piece(i):
            return pl.ds((i - 1) * CH, pieces[i][1].size)

        def places(h, a, b):
            return (a, b) if h == 0 else (b, a)

        def own_sums(p, d, h, i):
            return Fd[p, d, pl.ds(h * SUB, SUB), down_piece(i)] if i else Fg[p, d, :, pl.ds(h * CH, CH)]

        def near(u, a):
            return a + 1 - a % PAIR * PAIR if u == 0 else S - 1 - a

        def far(u, a):
            return near(1 - u, a)

        def rs_send(k):
            l, c = item(k)
            p = k % SLOTS
            for h in range(HALVES):
                a, b = places(h, px, py)
                for u in range(HALVES):
                    src = s1.at[p, h, pl.ds(1 + (a + u) % PAIR, PAIR), pl.ds(u * PAIR, PAIR)]
                    send(src, rA.at[l, c, h, u], rs_s.at[0, p], rs_r.at[k, 0], at(*places(h, near(u, a), b)))

        def rs_pass_b(k):
            p = k % SLOTS

            @pl.when((k >= 2) & (k < NI + 2))
            def _():
                for h in range(HALVES):
                    a, b = places(h, px, py)
                    for u in range(HALVES):
                        src = sb.at[p, h, pl.ds(u * PAIR, PAIR)]
                        send(src, lb.at[(k - 2) % NW, h, u], rs_s.at[1, p], rs_r.at[k - 2, 1], at(*places(h, far(u, a), b)))

        def rs_pass_2(k):
            p = k % SLOTS

            @pl.when((k >= 3) & (k < NI + 3))
            def _():
                for h in range(HALVES):
                    a, b = places(h, px, py)
                    for r in range(1, S):
                        to = at(*places(h, a, b + r))
                        send(s2.at[1 - p, h, (b + r) % S], l2.at[1 - p, h, S - 1 - r], rs_s.at[2, 1 - p], rs_r.at[k - 3, 2], to)

        def rs_early(k):
            @pl.when((k >= 2) & (k < NI + 2))
            def _():
                l, c = item(k - 2)
                wait(rA.at[l, c], rs_r.at[k - 2, 0])
                wait(rA.at[l, c], rs_s.at[0, k % SLOTS])
                pltpu.make_async_copy(rA.at[l, c], la, rs_l).start()

        def rs_arrived_a(k):
            pl.when((k >= 2) & (k < NI + 2))(lambda: wait(la, rs_l))

        def rs_arrived(k):
            for stage_of, here in ((1, lb), (2, l2)):
                q = k - 2 - stage_of

                @pl.when((q >= 0) & (q < NI))
                def _():
                    wait(here.at[0], rs_r.at[q, stage_of])
                    wait(here.at[0], rs_s.at[stage_of, q % SLOTS])

        def landed(k, lag, slots):
            any_yet = (k + NI + 4 - lag) // (NI + 4)
            return any_yet * ((k + NI - lag) % slots) + (1 - any_yet) * (slots - 1)

        def rs_sums(k):
            in_b, in_2 = landed(k, 3, NW), landed(k, 4, SLOTS)
            q = (k + NI - 4) % NI
            l, c = item(q)
            p = k % SLOTS
            squares = jnp.zeros(TILE, f32)
            for h in range(HALVES):
                for i, piece in enumerate(pieces):
                    total = o2[(h,) + piece]
                    for j in range(S - 1):
                        total += l2[(in_2, h, j) + piece].astype(f32)
                    g = total.astype(bf16)
                    if i:
                        gd[l, pl.ds(pl.multiple_of(c * RC + h * SUB, SUB), SUB), down_piece(i)] = g
                    else:
                        (gg, gu)[h][l, :, cols(c)] = g
                    g = g.astype(f32)
                    g = g * g
                    for a in range(g.shape[0] // SUB):
                        for b in range(g.shape[1] // LANES):
                            squares += g[a * SUB : (a + 1) * SUB, b * LANES : (b + 1) * LANES]
            acc[...] += jnp.where(k >= 4, squares, 0.0)
            for h in range(HALVES):
                a, b = places(h, px, py)
                for i, piece in enumerate(pieces):
                    for s in range(S):
                        total = o1[(1 - p, h, s) + piece] + lb[(in_b, h, s // PAIR, s % PAIR) + piece].astype(f32)
                        s2[(1 - p, h, s) + piece] = total.astype(bf16)
                        own = jnp.where(b == s, total, own) if s else total
                    o2[(h,) + piece] = own

        def rs_sums_a(k):
            p = k % SLOTS
            for h in range(HALVES):
                a, b = places(h, px, py)
                for i, piece in enumerate(pieces):
                    for s in range(S):
                        u = s // PAIR
                        ours = (a + 1 + u) % PAIR
                        for keep_it, first, index in ((True, a, ours), (False, far(u, a), 1 - ours)):
                            ix, iy = places(h, first, s)
                            total = own_sums(p, ix * S + iy, h, i) + la[(h, u, index, s % PAIR) + piece].astype(f32)
                            if keep_it:
                                o1[(p, h, s) + piece] = total
                            else:
                                sb[(p, h, s) + piece] = total.astype(bf16)

        def load_hidden(k):
            l, c = item(k)
            for d in range(n):
                rows = hid_h.at[l, pl.ds(pl.multiple_of(d * RF + c * RC, 8), RC)]
                pltpu.make_async_copy(rows, hid.at[pl.ds(d * RC, RC)], shid.at[0]).start()

        def at_rows(slot, row, size):
            return pl.ds(row % CH, size), pl.ds(pl.multiple_of(slot * (T // 2) + row // CH * TD, TD), TD)

        def each_h(b, do):
            size = LANES
            for row in range(0, D, size):
                do(pltpu.make_async_copy(h1_h.at[pl.ds(row, size), blocks(b, TD)], hid.at[at_rows(b % SLOTS, row, size)], sh.at[b % SLOTS]))

        def through_norm():
            def block(b, _):
                t = blocks(b, TD)
                pl.when((b > 0) & (b + 1 < NB))(lambda: each_h(b + 1, lambda copy: copy.start()))
                each_h(b, lambda copy: copy.wait())

                def both(g):
                    rows = pl.ds(g, PACK)
                    return daT[rows, t].astype(bf16).astype(f32), hid[at_rows(b % SLOTS, g, PACK)].astype(f32)

                along = jnp.zeros((SUB, TD), f32)
                for g in range(0, D, PACK):
                    da, wide = both(g)
                    wide = da * wide
                    along += wide[:SUB] + wide[SUB:]
                scale = scl[:, t]
                along = jnp.sum(along, axis=0, keepdims=True) * (scale * scale * scale) * (-1 / D)
                for g in range(0, D, PACK):
                    da, wide = both(g)
                    dyT[pl.ds(g, PACK), t] += (da * scale + wide * along).astype(bf16)
                return 0

            lax.fori_loop(0, NB, block, 0)
            load_hidden(NC)

        load_hidden(0)

        def one(k, _):
            l, c = item(k)
            slot = k % SLOTS

            @pl.when(k + 1 < NI)
            def _():
                load_wd(*item(k + 1), 1 - slot).start()

            @pl.when(k == NC)
            def _():
                through_norm()
                wait(aT, sm.at[0])

            @pl.when(k + 1 < NC)
            def _():
                load_w((L - 1) * NC + k + 1, 1 - slot)

            rs_early(k)
            load_wd(l, c, slot).wait()

            def block(j, _):
                load_stage(k, j).wait()
                t = blocks(j, TB)
                dh = dot(wdc[slot], dyT[:, t]).astype(bf16).astype(f32)
                big[:CH, t] = (dh * stage[j, CH:, :]).astype(bf16)
                big[CH:, t] = (dh * stage[j, :CH, :]).astype(bf16)
                pl.when(k + 1 < NI)(lambda: load_stage(k + 1, j).start())
                return 0

            lax.fori_loop(0, NJ, block, 0)
            rs_arrived_a(k)
            rs_arrived(k)
            rs_sums(k)
            rs_sums_a(k)

            def to_send(d, h):
                first, second = places(h, d // S, d % S)
                return slot, h, (first + S - (px, py)[h]) % S, second

            wide = dot(aT[...], big[...], NT)
            for d in range(n):
                block = wide[d * R : (d + 1) * R]
                Fg[slot, d] = block
                for h in range(HALVES):
                    s1[to_send(d, h) + pieces[0]] = block[:, h * CH : (h + 1) * CH].astype(bf16)
            rs_pass_b(k)
            rs_pass_2(k)
            pl.when(k == NC - 1)(lambda: pltpu.make_async_copy(a0_h, aT, sm.at[0]).start())
            wait(hid, shid.at[0])

            @pl.when(k < NI)
            def _():
                down = dot(dyT[...], hid[...], NT).T
                for d in range(n):
                    block = down[d * RC : (d + 1) * RC]
                    Fd[slot, d] = block
                    for h in range(HALVES):
                        for i in range(1, len(pieces)):
                            columns = down_piece(i)
                            some = block[h * SUB : (h + 1) * SUB, columns.start : columns.start + columns.size]
                            s1[to_send(d, h) + pieces[i]] = some.astype(bf16)

            rs_send(k)
            pl.when((k + 1 < NI) & (k + 1 != NC))(lambda: load_hidden(k + 1))

            @pl.when(k + 1 == NC)
            def _():
                for b in range(2):
                    each_h(b, lambda copy: copy.start())


            def into(first):
                wait_w(slot)
                da = dot(wcomb[slot].reshape(D, WIDE), big[...])
                daT[...] = da if first else daT[...] + da

            pl.when(k == 0)(lambda: into(True))
            pl.when((k > 0) & (k < NC))(lambda: into(False))
            return 0

        lax.fori_loop(0, NI, one, 0)

        def rest(k, _):
            rs_early(k)
            rs_arrived_a(k)
            rs_sums_a(k)
            rs_pass_b(k)
            rs_arrived(k)
            rs_sums(k)
            rs_pass_2(k)
            return 0

        lax.fori_loop(NI, NI + 4, rest, 0)

    pl.run_scoped(
        backward,
        vmem((D, T), f32),
        vmem((WIDE, T), bf16),
        vmem((n * RC, T), bf16),
        vmem((SLOTS, n, R, WIDE), f32),
        vmem((SLOTS, n, RC, D), f32),
        vmem((SLOTS, HALVES, S, S, RB, CH), bf16),
        vmem((SLOTS, HALVES, S, RB, CH), bf16),
        vmem((SLOTS, HALVES, S, RB, CH), bf16),
        vmem((SLOTS, HALVES, S, RB, CH), f32),
        vmem((HALVES, RB, CH), f32),
        vmem(rA.shape[2:], bf16),
        dma((SLOTS,)),
    )

    results = [pltpu.make_async_copy(here, to, sm.at[i]) for i, (here, to) in enumerate(((gg, gg_h), (gu, gu_h), (gd, gd_h)))]
    for copy in results:
        copy.start()
    sst[...] = acc[...]
    ssr[me] = acc[...]
    for r in range(1, n):
        send(sst, ssr.at[me], ss_s, ss_r, {"dp": (me + r) % n})
    wait(ssr.at[pl.ds(0, n - 1)], ss_r)
    wait(ssr.at[pl.ds(0, n - 1)], ss_s)
    total = ssr[0]
    for d in range(1, n):
        total += ssr[d]
    ss[...] = total
    for copy in results:
        copy.wait()


def solution(mesh):
    n = mesh.shape["dp"]
    S = math.isqrt(n)

    def step(x, dy, *arrays):
        weights, m, v = (arrays[i : i + 3] for i in (0, 3, 6))
        L, R, FF = weights[0].shape
        RF, D = weights[2].shape[1:]
        T = x.shape[1]
        NC = FF // CH
        RB = R + SUB * pl.cdiv(D, CH)
        NJ = T // TB
        sds = jax.ShapeDtypeStruct
        vmem, dma = pltpu.VMEM, pltpu.SemaphoreType.DMA
        outs = [
            (sds((L, R, FF), bf16), pl.ANY),
            (sds((L, R, FF), bf16), pl.ANY),
            (sds((L, RF, D), bf16), pl.ANY),
            (sds(TILE, f32), pltpu.VMEM),
            (sds((2, L, NC, S, S, R, CH), bf16), pl.ANY),
            (sds((L, FF, D), bf16), pl.ANY),
            (sds((L, NC, WIDE, T), f32), pl.ANY),
            (sds((L, FF, T), bf16), pl.ANY),
            (sds((D, T), bf16), pl.ANY),
            (sds((D, T), bf16), pl.ANY),
            (sds((L, NC, HALVES, HALVES, PAIR, PAIR, RB, CH), bf16), pl.ANY),
        ]
        scratch = [
            vmem((L, R, FF), bf16),
            vmem((L, R, FF), bf16),
            vmem((L, RF, D), bf16),
            vmem((SLOTS, D, T), bf16),
            vmem((NJ, WIDE, TB), f32),
            vmem((SLOTS, S, S, R, WIDE), bf16),
            vmem((SLOTS, CH, D), bf16),
            vmem((1, T), f32),
            vmem(TILE, f32),
            vmem(TILE, f32),
            vmem((n,) + TILE, f32),
            vmem((3, HALVES, HALVES, PAIR, RB, CH), bf16),
            vmem((SLOTS, HALVES, S - 1, RB, CH), bf16),
            dma((SLOTS,)),
            dma((2, 2)),
            dma((SLOTS,)),
            dma((NJ,)),
            dma((SLOTS,)),
            dma((3,)),
            dma((AHEAD, 2)),
            dma((3, AHEAD, 2)),
            dma((3, L * NC, 2)),
            dma((3, SLOTS)),
            dma((L * NC, 3)),
            dma(()),
            dma(()),
            dma(()),
        ]
        flops = 15 * 2 * T * D * FF
        done = pl.pallas_call(
            lambda *refs: step_kernel(n, *refs),
            in_specs=[pl.BlockSpec(memory_space=pl.ANY)] * 5,
            out_specs=[pl.BlockSpec(memory_space=space) for _, space in outs],
            out_shape=[shape for shape, _ in outs],
            scratch_shapes=scratch,
            compiler_params=pltpu.CompilerParams(collective_id=0, has_side_effects=True, vmem_limit_bytes=VMEM_BYTES),
            cost_estimate=pl.CostEstimate(flops=flops, bytes_accessed=400 << 20, transcendentals=0),
            name="train_step",
        )(x[0], dy[0], *weights)
        gradients = done[:3]
        count = n * sum(g.size for g in gradients)
        old = [array for g, w, m_, v_ in zip(gradients, weights, m, v, strict=True) for array in (g, w, m_, v_)]
        new = pl.pallas_call(
            lambda *refs: adamw_kernel(count, *refs),
            in_specs=[pl.BlockSpec(memory_space=pltpu.VMEM)] + [pl.BlockSpec(memory_space=pl.ANY)] * len(old),
            out_specs=[pl.BlockSpec(memory_space=pl.ANY)] * (len(weights) * 3),
            out_shape=[sds(a.shape, a.dtype) for w, m_, v_ in zip(weights, m, v, strict=True) for a in (w, m_, v_)],
            scratch_shapes=[vmem(a.shape, a.dtype) for a in old] + [dma((len(old),))],
            compiler_params=pltpu.CompilerParams(vmem_limit_bytes=VMEM_BYTES),
            name="adamw",
        )(done[3], *old)
        return tuple(new[i] for which in range(3) for i in range(which, len(new), 3))

    states, cut = P(("rep", "dp"), None, None), P(None, "dp", None)
    return jax.shard_map(
        step,
        mesh=mesh,
        in_specs=(states, states) + (cut,) * 9,
        out_specs=(P("rep", "dp", None),) * 9,
        check_vma=False,
    )
```

time: 964 us -> 421 us (0.44)
  matrix products: 474 us -> 0 us
  Pallas kernels: 0 us -> 419 us
  waiting for transfers between devices: 367 us -> 0 us
  blocking collectives: 38.7 us -> 0 us
  local copies, waits for them, and re-layouts: 30.8 us -> 0 us
  other arithmetic: 28.9 us -> 0 us
  between operations: 17.2 us -> 0.81 us
    dot_general x15 -> x0, matrix products: 474 us -> none  [the longest x5 173 us: layer(): up = jnp.dot(a, w['w_up'], preferred_element_type=jnp.float32)]
    pallas_call x0 -> x2, Pallas kernels: none -> 419 us  [the longest x1 412 us: step(): pl.pallas_call(lambda *refs: step_kernel(n, *refs), in_specs=[pl.BlockSpe...]
    unnamed x18 -> x0, waiting for transfers between devices: 257 us -> none
    all_gather x6 -> x0, waiting for transfers between devices: 109 us -> none  [fetched(): lax.all_gather(w[number], 'dp', axis=0, tiled=True)]
    psum x1 -> x0, blocking collectives: 38.7 us -> none  [step(): squares = lax.psum(sum((jnp.sum(g * g) for g in gradients)), 'dp')]
    unnamed x24 -> x0, local copies, waits for them, and re-layouts: 25.1 us -> none
    reduce_sum x4 -> x0, other arithmetic: 10.4 us -> none  [the longest x3 5.83 us: step(): squares = lax.psum(sum((jnp.sum(g * g) for g in gradients)), 'dp')]
    add_any x1 -> x0, other arithmetic: 9.79 us -> none  [normed(): wide = h.astype(jnp.float32)]
  transfers between devices with their start and end apart: 12 -> 0, of which waited for: 10 -> 0; matrix products, arithmetic and copies ran while one was open for 39% -> 0% of each run, Pallas kernels for 0% -> 0%
where the time goes in v1:
time: 421 us; the launch traced here: 420 us
  Pallas kernels  419 us (100%)
    pallas_call x1, Pallas kernels, step(): pl.pallas_call(lambda *refs: step_kernel(n, *refs), in_specs=[pl.BlockSpe...  412 us

profile of v1, /device:TPU:96, one launch (start us, length us, event | category | flops | bytes accessed | tf_op | source)
XLA Modules:
  0.0 420.0 jit_solution(769063087572286452)
XLA Ops:
  0.6 412.0 %train_step.1 = (bf16[2,56,2304]{2,1,0:T(8,128)(2,1)}, bf16[2,56,2304]{2,1,0:T(8,128)(2,1)}, bf16[2,144,896]{2,1,0:T(8,128)(2,1)}, f32[8,128]{1,0:T(8,128)}, bf1...) custom-call(bf16[4096,896]{1,0:T(8,128)(2,1)} %bitcast.2, ...), custom_call_target="tpu_custom_call" | custom-call | flops 253671505920 | bytes 419430400 | tf_op jit(solution)/shard_map/train_step/pallas_call | solution.py:709
  412.7 7.2 %adamw.1 = (bf16[2,56,2304]{2,1,0:T(8,128)(2,1)}, f32[2,56,2304]{2,1,0:T(8,128)}, f32[2,56,2304]{2,1,0:T(8,128)}, bf16[2,56,2304]{2,1,0:T(8,128)(2,1)}, f32[2,56...) custom-call(f32[8,128]{1,0:T(8,128)} %get-tuple-element.22.refs_0_, ...), custom_call_target="tpu_custom_call" | custom-call | tf_op jit(solution)/shard_map/adamw/pallas_call | solution.py:722
